TPU v7x, 32 devices: a whole 2x2x4 slice. The times are simulated.
32 devices in a mesh: replica: 8 (over y, x, core), mp: 4 (over z).
Axes of the slice: x: 2, y: 2, z: 4, core: 2. Of those that a mesh axis runs over, the one named last changes fastest.
Arguments:
- pseudo_grad: bfloat16 [8, 2, 3072, 2048], P('replica', None, None, 'mp'), may hold values from -6 to 6
- outer_params: float32 [2, 3072, 2048], P(None, 'replica', 'mp'), may hold values from -6 to 6
- momentum: float32 [2, 3072, 2048], P(None, 'replica', 'mp'), may hold values from -3 to 3
- acts: bfloat16 [1024, 3072], P('replica', 'mp'), may hold values from -6 to 6
- queries: bfloat16 [1024, 2048], P('replica', 'mp'), may hold values from -6 to 6
- keys: bfloat16 [1024, 2048], P('replica', 'mp'), may hold values from -6 to 6
- doc_ids: int32 [1024], P('replica'), may hold values from 0 to 31, never falling along the last dimension, each value on 1 to 64 neighbouring positions
Outputs:
- new_outer: float32 [2, 3072, 2048], P(None, 'replica', 'mp')
- new_momentum: float32 [2, 3072, 2048], P(None, 'replica', 'mp')
- new_local: bfloat16 [8, 3072, 2048], P('replica', None, 'mp')
Inputs may be any that keep to these rules, and one draw needn't show every extreme that they name: doc_ids never fall along the rows; each document covers 1 to 64 positions.
All inputs are finite; a program needn't handle non-finite values.
Results may differ from a plain program's by a relative error of at most 0.0037.
The roundings to bfloat16 on the way count: a program that leaves them out, or rounds other values in their place, can miss the bound.
Values may be sent and summed in bfloat16 or wider, within the bound.
A program may use at most 64 MiB of HBM per device.

v0:
```python
import jax
import jax.numpy as jnp
from jax import lax
from jax.sharding import PartitionSpec as P

HD = 256


norm_eps = 1e-06
outer_rate = 0.7
outer_beta = 0.9
inner_rate = 0.1


def attend(query, key_rows, value_rows, doc_rows):
    count = query.shape[0]
    scores = jnp.einsum(
        "qhd,khd->hqk", query, key_rows, preferred_element_type=jnp.float32
    ) * query.shape[2] ** (-0.5)
    row_pos = lax.broadcasted_iota(jnp.int32, (count, count), 0)
    col_pos = lax.broadcasted_iota(jnp.int32, (count, count), 1)
    allowed = (row_pos >= col_pos) & (doc_rows[:, None] == doc_rows[None, :])
    scores = jnp.where(allowed[None], scores, -1e30)
    probs = jax.nn.softmax(scores, axis=-1).astype(jnp.bfloat16)
    context = jnp.einsum("hqk,khd->qhd", probs, value_rows, preferred_element_type=jnp.float32)
    return context.astype(jnp.bfloat16)


def outer_update(summed, params_rows, moment_rows, workers):
    delta = summed / workers
    moment_next = outer_beta * moment_rows + delta
    params_next = params_rows - outer_rate * (delta + outer_beta * moment_next)
    return (params_next, moment_next)


def shards(pseudo_grad, outer_params, momentum, acts, queries, keys, doc_ids):
    workers = lax.axis_size("replica")
    groups = lax.axis_size("mp")
    full_x = lax.all_gather(acts, "mp", axis=1, tiled=True)
    blocks = lax.all_to_all(pseudo_grad, "replica", split_axis=2, concat_axis=0, tiled=True)
    summed = jnp.sum(blocks.astype(jnp.float32), axis=0)
    new_outer, new_momentum = outer_update(summed, outer_params, momentum, workers)
    weights = lax.all_gather(new_outer.astype(jnp.bfloat16), "replica", axis=1, tiled=True)
    count, width = full_x.shape
    cols = weights.shape[2]
    heads_here = cols // HD
    all_cols = cols * groups
    rows_f = full_x.astype(jnp.float32)
    normed = (
        rows_f * lax.rsqrt(jnp.mean(rows_f * rows_f, axis=-1, keepdims=True) + norm_eps)
    ).astype(jnp.bfloat16)
    values = (
        jnp.dot(normed, weights[0], preferred_element_type=jnp.float32) * width ** (-0.5)
    ).astype(jnp.bfloat16)
    query = queries.reshape(count, heads_here, HD)
    keyed = keys.reshape(count, heads_here, HD)

    def attn_fn(c):
        return attend(query, keyed, c, doc_ids)

    context, pullback = jax.vjp(attn_fn, values.reshape(count, heads_here, HD))
    ctx = context.reshape(count, cols)
    partial_branch = lax.dot_general(
        ctx, weights[1], (((1,), (1,)), ((), ())), preferred_element_type=jnp.float32
    ) * all_cols ** (-0.5)
    branch = lax.psum(partial_branch.astype(jnp.bfloat16), "mp").astype(jnp.float32)
    dout = (rows_f + branch - jnp.roll(rows_f, -1, axis=0)).astype(jnp.bfloat16)
    dctx = (
        jnp.dot(dout, weights[1], preferred_element_type=jnp.float32) * all_cols ** (-0.5)
    ).astype(jnp.bfloat16)
    pulled = pullback(dctx.reshape(count, heads_here, HD))[0]
    grad = lax.dot_general(
        normed,
        pulled.reshape(count, cols),
        (((0,), (0,)), ((), ())),
        preferred_element_type=jnp.float32,
    ) * width ** (-0.5)
    squares = lax.psum(jnp.sum(grad * grad), "mp")
    rms = jnp.sqrt(squares / (width * all_cols) + norm_eps)
    new_local = (weights[0].astype(jnp.float32) - inner_rate * grad / rms).astype(jnp.bfloat16)
    return (new_outer, new_momentum, new_local[None])


def solution(mesh):
    placed = (
        P("replica", None, None, "mp"),
        P(None, "replica", "mp"),
        P(None, "replica", "mp"),
        P("replica", "mp"),
        P("replica", "mp"),
        P("replica", "mp"),
        P("replica"),
    )
    return jax.shard_map(
        shards,
        mesh=mesh,
        in_specs=placed,
        out_specs=(P(None, "replica", "mp"), P(None, "replica", "mp"), P("replica", None, "mp")),
        check_vma=False,
    )
```

profile of v0, /device:TPU:0, one launch (start us, length us, event | category | flops | bytes accessed | tf_op | source)
XLA Modules:
  0.0 232.5 jit_solution(10670747100160510871)
XLA Ops:
  7.2 0.0 all-gather.2.cloned.1.call-start
  7.2 11.1 %copy.23 = bf16[1,2,3072,512]{3,1,0,2:T(2,128)(2,1)S(1)} copy(bf16[1,2,3072,512]{3,2,1,0:T(8,128)(2,1)} %param.7) | data formatting | bytes 12582912 | tf_op args[0]
  18.3 76.5 %all_to_all.4 = bf16[1,2,3072,512]{3,1,0,2:T(2,128)(2,1)S(1)} all-to-all(bf16[1,2,3072,512]{3,1,0,2:T(2,128)(2,1)S(1)} %copy.23), channel_id=1, replica_groups=mesh['replica'=8,'mp'=4] {'replica'}, dimensions={2} | all-to-all | bytes 12582912 | tf_op jit(solution)/shard_map/all_to_all | solution.py:40
  94.8 6.3 %convert_reduce_fusion = f32[2,384,512]{2,0,1:T(2,128)S(1)} fusion(bf16[2,8,384,512]{3,0,2,1:T(2,128)(2,1)S(1)} %bitcast.46), kind=kLoop, calls=%fused_computation.1 | loop fusion | flops 5898240 | bytes 7864320 | tf_op jit(solution)/shard_map/reduce_sum | solution.py:41
  101.1 0.0 copy-done
  101.1 0.0 copy-done.1
  101.1 0.0 copy-start.3
  101.1 0.0 copy-start.4
  101.1 0.0 copy-start.5
  101.1 0.0 copy-start.2
  101.1 2.7 %fusion.21 = (bf16[2,384,512]{2,1,0:T(8,128)(2,1)}, f32[2,384,512]{2,1,0:T(8,128)}, f32[2,384,512]{2,1,0:T(8,128)}) fusion(f32[2,384,512]{2,1,0:T(8,128)S(1)} %copy-done, f32[2,384,512]{2,0,1:T(2,128)S(1)} %convert_reduce_fusion, f32[2,384,512]{2,1,0:T(8,128)S(1)} %copy-done.1), kind=kLoop, calls=%fused_computation.38 | loop fusion | flops 3145728 | bytes 8650752 | tf_op jit(solution)/shard_map/convert_element_type | solution.py:43
  103.8 0.0 all-gather.2.cloned.1.call-update
  103.8 0.0 all-reduce.2.cloned.1.call-start
  103.9 0.1 fusion.19
  104.0 0.2 fusion.12
  104.2 0.1 fusion.22
  104.3 19.8 %all_gather.7 = bf16[128,3072]{1,0:T(8,128)(2,1)S(1)} all-gather(bf16[128,768]{1,0:T(8,128)(2,1)S(1)} %copy-done.2), channel_id=1, replica_groups=mesh['replica'=8,'mp'=4] {'mp'}, dimensions={1}, use_global_device_ids=true | all-gather | bytes 983040 | tf_op jit(solution)/shard_map/all_gather | solution.py:39
  124.1 0.2 multiply_reduce_fusion.1
  124.3 24.4 %all-gather.2.cloned.1.call-done = bf16[2,3072,512]{2,1,0:T(8,128)(2,1)} async-done(((bf16[2,384,512]{2,1,0:T(8,128)(2,1)}), bf16[2,3072,512]{2,1,0:T(8,128)(2,1)}) %all-gather.2.cloned.1.call-update) | async-done | bytes 6291472 | tf_op jit(solution)/shard_map/all_gather | solution.py:43
  148.7 2.5 %fusion.9 = bf16[128,512]{1,0:T(8,128)(2,1)S(1)} fusion(bf16[2,3072,512]{2,1,0:T(8,128)(2,1)} %all-gather.2.cloned.1.call-done, bf16[128,3072]{1,0:T(8,128)(2,1)S(1)} %all_gather.7, f32[128]{0:T(128)S(1)} %add_rsqrt_fusion), kind=kOutput, calls=%fused_computation.23 | convolution fusion | flops 403963904 | bytes 4063744 | tf_op jit(solution)/shard_map/dot_general | solution.py:53
  151.3 0.1 copy.33
  151.4 0.2 convolution_convert_fusion.1
  151.6 3.9 %fusion.1 = bf16[128,3072]{1,0:T(8,128)(2,1)} fusion(bf16[128,512]{0,1:T(8,128)(2,1)S(1)} %bitcast.52, bf16[2,3072,512]{2,1,0:T(8,128)(2,1)} %all-gather.2.cloned.1.call-done), kind=kOutput, calls=%fused_computation.5 | convolution fusion | flops 403439616 | bytes 4063232 | tf_op jit(solution)/shard_map/dot_general | solution.py:63
  155.5 0.0 all-reduce.2.cloned.1.call-update
  155.6 0.2 slice.22
  155.8 43.8 %all-reduce.2.cloned.1.call-done = bf16[128,3072]{1,0:T(8,128)(2,1)} async-done(((bf16[128,3072]{1,0:T(8,128)(2,1)}), bf16[128,3072]{1,0:T(8,128)(2,1)}) %all-reduce.2.cloned.1.call-update) | async-done | bytes 786448 | tf_op jit(solution)/shard_map/psum | solution.py:66
  199.6 2.8 %fusion.10 = bf16[128,512]{1,0:T(8,128)(2,1)S(1)} fusion(bf16[2,3072,512]{2,1,0:T(8,128)(2,1)} %all-gather.2.cloned.1.call-done, f32[1,3072]{1,0:T(1,128)S(1)} %slice.23, f32[127,3072]{1,0:T(8,128)S(1)} %slice.22, bf16[128,3072]{1,0:T(8,128)(2,1)} %all-reduce.2.cloned.1.call-done, bf16[128,3072]{1,0:T(8,128)(2,1)S(1)} %all_gather.7), kind=kOutput, calls=%fused_computation.24 | convolution fusion | flops 405143552 | bytes 6422528 | tf_op jit(solution)/shard_map/dot_general | solution.py:69
  202.4 0.1 copy.34
  202.5 0.2 convolution_convert_fusion
  202.7 5.1 %multiply_reduce_fusion = (f32[]{:T(128)}, f32[3072,512]{1,0:T(8,128)}) fusion(bf16[128,512]{0,1:T(8,128)(2,1)S(1)} %bitcast.47, bf16[128,3072]{1,0:T(8,128)(2,1)S(1)} %all_gather.7, f32[128]{0:T(128)S(1)} %add_rsqrt_fusion), kind=kOutput, calls=%fused_computation.3 | convolution fusion | flops 408551424 | bytes 7209476 | tf_op jit(solution)/shard_map/dot_general | solution.py:72
  207.8 10.6 %psum.15 = f32[]{:T(128)} all-reduce(f32[]{:T(128)} %get-tuple-element.6), channel_id=1, replica_groups=mesh['replica'=8,'mp'=4] {'mp'}, use_global_device_ids=true, to_apply=%region_6.7 | all-reduce | flops 1 | bytes 8 | tf_op jit(solution)/shard_map/psum | solution.py:78
  219.1 6.5 %fusion.2 = bf16[1,3072,512]{2,1,0:T(8,128)(2,1)} fusion(f32[]{:T(128)S(6)} %sqrt.3, f32[3072,512]{1,0:T(8,128)} %get-tuple-element.7, bf16[2,3072,512]{2,1,0:T(8,128)(2,1)} %all-gather.2.cloned.1.call-done), kind=kLoop, calls=%fused_computation.8 | loop fusion | flops 7864320 | bytes 12582916 | tf_op jit(solution)/shard_map/broadcast_in_dim | solution.py:81
  (8 shorter events, 0.0 us)
Async XLA Ops:
  7.2 141.6 %all-gather.2.cloned.1.call-start = ((), (), s32[]{:S(2)}) async-start(), calls=%async_computation.1 | async-start | bytes 7077888 | tf_op jit(solution)/shard_map/all_gather | solution.py:43
  94.8 6.3 %copy-start = (f32[2,384,512]{2,1,0:T(8,128)S(1)}, f32[2,384,512]{2,1,0:T(8,128)}, u32[]{:S(2)}) copy-start(f32[2,384,512]{2,1,0:T(8,128)} %param.8) | copy-start | bytes 4718596
  94.8 6.3 %copy-start.1 = (f32[2,384,512]{2,1,0:T(8,128)S(1)}, f32[2,384,512]{2,1,0:T(8,128)}, u32[]{:S(2)}) copy-start(f32[2,384,512]{2,1,0:T(8,128)} %param.9) | copy-start | bytes 4718596
  101.1 2.8 %copy-start.3 = (s32[128]{0:T(128)S(1)}, s32[128]{0:T(128)}, u32[]{:S(2)}) copy-start(s32[128]{0:T(128)} %param.13) | copy-start | bytes 1540
  101.1 2.9 %copy-start.4 = (bf16[128,512]{1,0:T(8,128)(2,1)S(1)}, bf16[128,512]{1,0:T(8,128)(2,1)}, u32[]{:S(2)}) copy-start(bf16[128,512]{1,0:T(8,128)(2,1)} %param.12) | copy-start | bytes 393220
  101.1 2.9 %copy-start.5 = (bf16[128,512]{1,0:T(8,128)(2,1)S(1)}, bf16[128,512]{1,0:T(8,128)(2,1)}, u32[]{:S(2)}) copy-start(bf16[128,512]{1,0:T(8,128)(2,1)} %param.11) | copy-start | bytes 393220
  101.1 3.1 %copy-start.2 = (bf16[128,768]{1,0:T(8,128)(2,1)S(1)}, bf16[128,768]{1,0:T(8,128)(2,1)}, u32[]{:S(2)}) copy-start(bf16[128,768]{1,0:T(8,128)(2,1)} %param.10) | copy-start | bytes 589828
  103.8 95.7 %all-reduce.2.cloned.1.call-start = ((), (), s32[]{:S(2)}) async-start(), calls=%async_computation.2 | async-start | bytes 1572864 | tf_op jit(solution)/shard_map/psum | solution.py:66
Sparse Core Ops, SparseCore 0:
  103.9 44.7 all-gather.1
  155.7 43.8 all-reduce.1
where the time goes:
time: 233 us; the launch traced here: 232 us
  blocking collectives  107 us (46%)
  waiting for transfers between devices  68.2 us (29%)
  other arithmetic  15.8 us (7%)
  matrix products  15 us (6%)
  between operations  14.9 us (6%)
  local copies, waits for them, and re-layouts  11.6 us (5%)
    all_to_all x1, blocking collectives, shards(): lax.all_to_all(pseudo_grad, 'replica', split_axis=2, concat_axis=0, tiled...  76.5 us
    psum x1, waiting for transfers between devices, shards(): lax.psum(partial_branch.astype(jnp.bfloat16), 'mp').astype(jnp.float32)  43.8 us
    all_gather x1, waiting for transfers between devices, shards(): lax.all_gather(new_outer.astype(jnp.bfloat16), 'replica', axis=1, tiled=T...  24.4 us
    all_gather x1, blocking collectives, shards(): full_x = lax.all_gather(acts, 'mp', axis=1, tiled=True)  19.8 us
    unnamed x13, local copies, waits for them, and re-layouts  11.1 us
    psum x1, blocking collectives, shards(): squares = lax.psum(jnp.sum(grad * grad), 'mp')  10.6 us
    broadcast_in_dim x1, other arithmetic, shards(): return (new_outer, new_momentum, new_local[None])  6.48 us
    reduce_sum x1, other arithmetic, shards(): summed = jnp.sum(blocks.astype(jnp.float32), axis=0)  6.26 us
  transfers between devices with their start and end apart: 2, of which 2 were waited for; matrix products, arithmetic and copies ran while one was open for 0% of the time, Pallas kernels for 0%

commit v1 on v0

v1 whole, which is shorter than its diff:
```python
import functools

import jax
import jax.numpy as jnp
from jax import lax
from jax.experimental import pallas as pl
from jax.experimental.pallas import tpu as pltpu
from jax.sharding import PartitionSpec as P

HD = 256
MESH = pl.DeviceIdType.MESH
F32 = jnp.float32
BF16 = jnp.bfloat16

norm_eps = 1e-06
outer_rate = 0.7
outer_beta = 0.9
inner_rate = 0.1


def bit_of(value, j):
    return (value // (1 << j)) % 2


def flip(value, mask, bits):
    out = value
    for j in range(bits):
        if (mask >> j) & 1:
            out = out + (1 - 2 * bit_of(value, j)) * (1 << j)
    return out


def row_tile(rows):
    for t in (64, 48, 32, 16):
        if rows % t == 0:
            return t
    return rows


def dot(a, b, ca, cb):
    return lax.dot_general(a, b, (((ca,), (cb,)), ((), ())), preferred_element_type=F32)


class Plan:
    def __init__(self, n, groups, rows, cols, count, width):
        self.n, self.groups, self.rows, self.cols, self.count, self.width = n, groups, rows, cols, count, width
        self.k = n.bit_length() - 1
        self.kz = groups.bit_length() - 1
        self.heads = cols // HD
        self.chunk = width // groups
        self.streams = [(m, h) for m in range(2) for h in range(self.heads)]
        k = self.k
        self.order = [[0] + list(range(1, k)) if h % 2 == 0 else [0] + list(range(k - 1, 0, -1)) for _, h in self.streams]


def kernel(pl_, pg, op, mo, acts, qs, ks, dcol, drow, out_o, out_m, out_l,
           mine, r0, snds, recvs, opv, mov, nov, nmv, w, xg, xd, nrm, nrt, probs,
           pb, zr, zs, db, lov, sq, sqr,
           mine_sem, in_sem, r0_sem, rs_sem, ag_send, ag_recv, x_sem, z_send, z_recv, g_send, g_recv, q_sem, out_sem):
    n, groups, R, cols, count, width = pl_.n, pl_.groups, pl_.rows, pl_.cols, pl_.count, pl_.width
    k, kz, chunk = pl_.k, pl_.kz, pl_.chunk
    me = lax.axis_index("replica")
    mz = lax.axis_index("mp")
    S = pl_.streams
    order = pl_.order
    T = row_tile(R)

    def rep(mask):
        return {"replica": flip(me, mask, k)}

    def zdev(mask):
        return {"mp": flip(mz, mask, kz)}

    b0 = bit_of(me, 0)

    def hs(h):
        return pl.ds(h * HD, HD)

    mine_cp = []
    for s, (m, h) in enumerate(S):
        c = pltpu.make_async_copy(pg.at[m, :, b0, :, hs(h)], mine.at[s], mine_sem.at[s])
        c.start()
        mine_cp.append(c)
    op_cp = pltpu.make_async_copy(op, opv, in_sem.at[0])
    mo_cp = pltpu.make_async_copy(mo, mov, in_sem.at[1])

    bar = pltpu.get_barrier_semaphore()
    for j in range(k):
        pl.semaphore_signal(bar, inc=1, device_id=rep(1 << j), device_id_type=MESH)
    for mask in range(1, groups):
        pl.semaphore_signal(bar, inc=1, device_id=zdev(mask), device_id_type=MESH)
    pl.semaphore_wait(bar, k + groups - 1)

    r0_cp = []
    for s, (m, h) in enumerate(S):
        c = pltpu.make_async_remote_copy(
            src_ref=pg.at[m, :, 1 - b0, :, hs(h)], dst_ref=r0.at[s],
            send_sem=r0_sem.at[0, s], recv_sem=r0_sem.at[1, s], device_id=rep(1), device_id_type=MESH)
        c.start()
        r0_cp.append(c)
    x_cp = []
    for mask in range(1, groups):
        c = pltpu.make_async_remote_copy(
            src_ref=acts, dst_ref=xg.at[mask], send_sem=x_sem.at[0, mask], recv_sem=x_sem.at[1, mask],
            device_id=zdev(mask), device_id_type=MESH)
        c.start()
        x_cp.append(c)
    op_cp.start()
    mo_cp.start()

    def level_up(s, t, u, bit):
        if order[s] == sorted(order[s]):
            return 2 * u + bit
        return bit * ((n // 2) >> t) + u

    def block_sum(s, t, u):
        idx = [(t, u)]
        cur = u
        for tt in range(t, 0, -1):
            cur = level_up(s, tt, cur, bit_of(me, order[s][tt]))
            idx.append((tt - 1, cur))

        def rows_at(rs):
            acc = None
            for tt, uu in reversed(idx):
                if tt == 0:
                    acc = mine[s, uu, rs, :].astype(F32) + r0[s, uu, rs, :].astype(F32)
                else:
                    acc = acc + recvs[tt - 1][s, uu, rs, :].astype(F32)
            return acc
        return rows_at

    rs_cp = {}

    def rs_stage(s, t):
        if t == 1:
            mine_cp[s].wait()
            r0_cp[s].wait_recv()
        else:
            rs_cp[s, t - 1].wait_recv()
        c = (n // 2) >> t
        other = 1 - bit_of(me, order[s][t])

        def body(i, _):
            u = i // (R // T)
            rs = pl.ds(pl.multiple_of((i % (R // T)) * T, T), T)
            val = block_sum(s, t - 1, level_up(s, t, u, other))(rs)
            snds[t - 1][s, u, rs, :] = val.astype(BF16)
            return 0
        lax.fori_loop(0, c * (R // T), body, 0)
        cp = pltpu.make_async_remote_copy(
            src_ref=snds[t - 1].at[s], dst_ref=recvs[t - 1].at[s],
            send_sem=rs_sem.at[0, t - 1, s], recv_sem=rs_sem.at[1, t - 1, s],
            device_id=rep(1 << order[s][t]), device_id_type=MESH)
        cp.start()
        rs_cp[s, t] = cp

    ag = {}

    def held(s, e):
        masks = [0]
        for b in order[s][::-1][:e]:
            masks = masks + [x ^ (1 << b) for x in masks]
        return masks

    def ag_send_block(s, mask, first):
        m, h = S[s]
        for e in range(first, k):
            i = held(s, e).index(mask)
            ref = w.at[m, flip(me, mask, k), :, hs(h)]
            cp = pltpu.make_async_remote_copy(
                src_ref=ref, dst_ref=ref, send_sem=ag_send.at[s, (1 << e) + i], recv_sem=ag_recv.at[s, (1 << e) + i],
                device_id=rep(1 << order[s][k - 1 - e]), device_id_type=MESH)
            cp.start()
            ag[s, e, i] = cp

    def ag_wait_block(s, e, i):
        m, h = S[s]
        mask = held(s, e)[i] ^ (1 << order[s][k - 1 - e])
        ref = w.at[m, flip(me, mask, k), :, hs(h)]
        pltpu.make_async_remote_copy(
            src_ref=ref, dst_ref=ref, send_sem=ag_send.at[s, (1 << e) + i], recv_sem=ag_recv.at[s, (1 << e) + i],
            device_id=rep(1 << order[s][k - 1 - e]), device_id_type=MESH).wait_recv()
        return mask

    def update(s):
        m, h = S[s]
        last = k - 1
        if last == 0:
            mine_cp[s].wait()
            r0_cp[s].wait_recv()
        else:
            rs_cp[s, last].wait_recv()

        def body(i, _):
            rs = pl.ds(pl.multiple_of(i * T, T), T)
            delta = block_sum(s, last, 0)(rs) / n
            mn = outer_beta * mov[m, rs, hs(h)] + delta
            on = opv[m, rs, hs(h)] - outer_rate * (delta + outer_beta * mn)
            nmv[m, rs, hs(h)] = mn
            nov[m, rs, hs(h)] = on
            w[m, me, rs, hs(h)] = on.astype(BF16)
            return 0
        lax.fori_loop(0, R // T, body, 0)

    of = [s for s, (m, h) in enumerate(S) if m == 0]
    oo = [s for s, (m, h) in enumerate(S) if m == 1]

    allowed = lax.broadcasted_iota(jnp.int32, (count, count), 0) >= lax.broadcasted_iota(jnp.int32, (count, count), 1)
    allowed = allowed & (dcol[...] == drow[...])
    for h in range(pl_.heads):
        sc = dot(qs[:, hs(h)], ks[:, hs(h)], 1, 1) * HD ** (-0.5)
        sc = jnp.where(allowed, sc, -1e30)
        ex = jnp.exp(sc - jnp.max(sc, axis=1, keepdims=True))
        probs[h] = (ex / jnp.sum(ex, axis=1, keepdims=True)).astype(BF16)

    for s in of + oo:
        if k > 1:
            rs_stage(s, 1)

    xg[0] = acts[...]
    for c in x_cp:
        c.wait_recv()
    ssum = jnp.zeros((count, 1), F32)
    for g in range(groups):
        xf = xg[g].astype(F32)
        ssum = ssum + jnp.sum(xf * xf, axis=1, keepdims=True)
    inv = lax.rsqrt(ssum / width + norm_eps)
    gram = jnp.zeros((count, count), F32)
    for g in range(groups):
        xf = xg[g].astype(F32)
        nb = (xf * inv).astype(BF16)
        nrm[g] = nb
        nrt[g] = nb.astype(F32).T.astype(BF16)
        gram = gram + dot(nb, nb, 1, 1)
        xd[g] = xf - pltpu.roll(xf, count - 1, 0)

    for t in range(2, k):
        for s in of + oo:
            rs_stage(s, t)

    op_cp.wait()
    mo_cp.wait()
    for s in of:
        update(s)
        ag_send_block(s, 0, 0)
    for s in oo:
        update(s)
    out_cp = [pltpu.make_async_copy(nov, out_o, out_sem.at[0]), pltpu.make_async_copy(nmv, out_m, out_sem.at[1])]
    for c in out_cp:
        c.start()

    def forward(group, e):
        for i in range(1 << e):
            for s in group:
                mask = ag_wait_block(s, e, i)
                if e + 1 < k:
                    ag_send_block(s, mask, e + 1)

    for e in range(k - 1):
        forward(of, e)
        if e == 0:
            for s in oo:
                ag_send_block(s, 0, 0)
    if k == 1:
        for s in oo:
            ag_send_block(s, 0, 0)
    forward(of, k - 1)

    def wrows(m, g):
        part = w[m, pl.ds(pl.multiple_of(g * (n // groups), n // groups), n // groups)]
        return part.reshape(chunk, cols)

    vals = jnp.zeros((count, cols), F32)
    for g in range(groups):
        vals = vals + dot(nrm[g], wrows(0, flip(mz, g, kz)), 1, 0)
    vals = (vals * width ** (-0.5)).astype(BF16)
    ctx = jnp.concatenate(
        [dot(probs[h], vals[:, h * HD:(h + 1) * HD], 1, 0).astype(BF16) for h in range(pl_.heads)], axis=1)

    scale = (cols * groups) ** (-0.5)
    per = n // groups
    kg = kz
    gme = me // per

    def gidx(c):
        return flip(gme, c, kg)

    size = [count >> t for t in range(kz + 1)]
    start = [0]
    for t in range(kz):
        start.append(start[-1] + bit_of(mz, t) * size[t + 1])
    zcp = {}

    def z_rows(c, t, lo, num):
        acc = pb[c, pl.ds(pl.multiple_of(lo, num), num), :].astype(F32)
        for tt in range(1, t + 1):
            acc = acc + zr[tt - 1][c, pl.ds(pl.multiple_of(lo - start[tt], num), num), :].astype(F32)
        return acc

    def z_reduce(c, t):
        if t == 0:
            pb[c] = (dot(ctx, wrows(1, gidx(c)), 1, 1) * scale).astype(BF16)
        else:
            zcp[c, t - 1].wait_recv()
        num = size[t + 1]
        lo = start[t] + (1 - bit_of(mz, t)) * num
        if t == 0:
            src = pb.at[c, pl.ds(pl.multiple_of(lo, num), num)]
        else:
            zs[t - 1][c] = z_rows(c, t, lo, num).astype(BF16)
            src = zs[t - 1].at[c]
        cp = pltpu.make_async_remote_copy(
            src_ref=src, dst_ref=zr[t].at[c], send_sem=z_send.at[t, c], recv_sem=z_recv.at[t, c],
            device_id=zdev(1 << t), device_id_type=MESH)
        cp.start()
        zcp[c, t] = cp

    gcp = {}

    def zheld(e):
        masks = [0]
        for t in range(kz - 1, kz - 1 - e, -1):
            masks = masks + [x ^ (1 << t) for x in masks]
        return masks

    def owner_rows(mask):
        dev = flip(mz, mask, kz)
        lo = 0
        for t in range(kz):
            lo = lo + bit_of(dev, t) * size[t + 1]
        return pl.ds(pl.multiple_of(lo, size[kz]), size[kz])

    def z_copy(c, mask, e, i):
        ref = db.at[c, owner_rows(mask)]
        return pltpu.make_async_remote_copy(
            src_ref=ref, dst_ref=ref, send_sem=g_send.at[c, (1 << e) + i], recv_sem=g_recv.at[c, (1 << e) + i],
            device_id=zdev(1 << (kz - 1 - e)), device_id_type=MESH)

    def z_send_block(c, mask, first):
        for e in range(first, kz):
            i = zheld(e).index(mask)
            cp = z_copy(c, mask, e, i)
            cp.start()
            gcp[c, e, i] = cp

    def z_finish(c):
        zcp[c, kz - 1].wait_recv()
        lo, num = start[kz], size[kz]
        tot = z_rows(c, kz, lo, num)
        xz = flip(gidx(c), 0, kz)
        tot = tot + xd[xmask(xz), pl.ds(pl.multiple_of(lo, num), num), :]
        db[c, pl.ds(pl.multiple_of(lo, num), num), :] = tot.astype(BF16)
        z_send_block(c, 0, 0)

    def xmask(z):
        out = 0
        for j in range(kz):
            out = out + ((bit_of(z, j) + bit_of(mz, j)) % 2) * (1 << j)
        return out

    def z_forward(c, e):
        for i in range(1 << e):
            mask = zheld(e)[i] ^ (1 << (kz - 1 - e))
            z_copy(c, mask, e, i).wait_recv()
            if e + 1 < kz:
                z_send_block(c, mask, e + 1)

    def z_step(c, j):
        if j < kz:
            z_reduce(c, j)
        elif j == kz:
            z_finish(c)
        elif j <= 2 * kz:
            z_forward(c, j - kz - 1)

    ready = set([0 if False else None])
    arrived = {s: 0 for s in oo}
    for e in range(k - 1):
        forward(oo, e)
    forward(oo, k - 1)

    steps = 2 * kz + 1
    for wave in range(groups + steps - 1):
        for c in range(groups):
            j = wave - c
            if 0 <= j < steps:
                z_step(c, j)

    dctx = jnp.zeros((count, cols), F32)
    for c in range(groups):
        dctx = dctx + dot(db[c], wrows(1, gidx(c)), 1, 0)
    dctx = (dctx * scale).astype(BF16)
    dv = jnp.concatenate(
        [dot(probs[h], dctx[:, h * HD:(h + 1) * HD], 0, 0).astype(BF16) for h in range(pl_.heads)], axis=1)

    part = jnp.sum(gram * dot(dv, dv, 1, 1), axis=0, keepdims=True) / width
    sq[...] = jnp.broadcast_to(part, (8, count))
    qcp = []
    for mask in range(1, groups):
        c = pltpu.make_async_remote_copy(
            src_ref=sq, dst_ref=sqr.at[mask], send_sem=q_sem.at[0, mask], recv_sem=q_sem.at[1, mask],
            device_id=zdev(mask), device_id_type=MESH)
        c.start()
        qcp.append(c)
    tot = sq[...]
    for i, c in enumerate(qcp):
        c.wait_recv()
        tot = tot + sqr[i + 1]
    total = jnp.sum(tot[0:1, :], axis=1, keepdims=True)
    total = jnp.maximum(total, 0.0) / (width * cols * groups)
    fac = (inner_rate * width ** (-0.5)) * lax.rsqrt(total + norm_eps)
    for g in range(groups):
        z = flip(mz, g, kz)
        grad = dot(nrt[g], dv, 1, 0)
        rows = pl.ds(pl.multiple_of(z * chunk, chunk), chunk)
        lov[rows, :] = (wrows(0, z).astype(F32) - grad * fac).astype(BF16)
        c = pltpu.make_async_copy(lov.at[rows], out_l.at[0, rows], out_sem.at[2 + g])
        c.start()
        out_cp.append(c)

    for c in out_cp:
        c.wait()
    for c in r0_cp + x_cp + qcp + list(rs_cp.values()) + list(ag.values()) + list(zcp.values()) + list(gcp.values()):
        c.wait_send()


def shards(pseudo_grad, outer_params, momentum, acts, queries, keys, doc_ids):
    n = lax.axis_size("replica")
    groups = lax.axis_size("mp")
    _, mats, width, cols = pseudo_grad.shape
    rows = outer_params.shape[1]
    count = acts.shape[0]
    plan = Plan(n, groups, rows, cols, count, width)
    k, kz, ns, chunk = plan.k, plan.kz, len(plan.streams), plan.chunk
    half = n // 2
    pg = pseudo_grad.reshape(mats, half, 2, rows, cols)
    vm, anym = pl.BlockSpec(memory_space=pltpu.VMEM), pl.BlockSpec(memory_space=pl.ANY)
    dma = pltpu.SemaphoreType.DMA
    scratch = [
        pltpu.VMEM((ns, half, rows, HD), BF16),
        pltpu.VMEM((ns, half, rows, HD), BF16),
        [pltpu.VMEM((ns, half >> t, rows, HD), BF16) for t in range(1, k)],
        [pltpu.VMEM((ns, half >> t, rows, HD), BF16) for t in range(1, k)],
        pltpu.VMEM((mats, rows, cols), F32),
        pltpu.VMEM((mats, rows, cols), F32),
        pltpu.VMEM((mats, rows, cols), F32),
        pltpu.VMEM((mats, rows, cols), F32),
        pltpu.VMEM((mats, n, rows, cols), BF16),
        pltpu.VMEM((groups, count, chunk), BF16),
        pltpu.VMEM((groups, count, chunk), F32),
        pltpu.VMEM((groups, count, chunk), BF16),
        pltpu.VMEM((groups, chunk, count), BF16),
        pltpu.VMEM((plan.heads, count, count), BF16),
        pltpu.VMEM((groups, count, chunk), BF16),
        [pltpu.VMEM((groups, count >> (t + 1), chunk), BF16) for t in range(kz)],
        [pltpu.VMEM((groups, count >> (t + 1), chunk), BF16) for t in range(1, kz)],
        pltpu.VMEM((groups, count, chunk), BF16),
        pltpu.VMEM((width, cols), BF16),
        pltpu.VMEM((8, count), F32),
        pltpu.VMEM((groups, 8, count), F32),
        dma((ns,)), dma((2,)), dma((2, ns)), dma((2, k, ns)), dma((ns, n)), dma((ns, n)),
        dma((2, groups)), dma((kz, groups)), dma((kz, groups)), dma((groups, groups)), dma((groups, groups)),
        dma((2, groups)), dma((2 + groups,)),
    ]
    return pl.pallas_call(
        functools.partial(kernel, plan),
        out_shape=(
            jax.ShapeDtypeStruct(outer_params.shape, F32),
            jax.ShapeDtypeStruct(momentum.shape, F32),
            jax.ShapeDtypeStruct((1, width, cols), BF16),
        ),
        in_specs=[anym, anym, anym, vm, vm, vm, vm, vm],
        out_specs=(anym, anym, anym),
        scratch_shapes=scratch,
        compiler_params=pltpu.CompilerParams(
            collective_id=0, has_side_effects=True, vmem_limit_bytes=62 * 1024 * 1024),
    )(pg, outer_params, momentum, acts, queries, keys, doc_ids.reshape(count, 1), doc_ids.reshape(1, count))


def solution(mesh):
    placed = (
        P("replica", None, None, "mp"),
        P(None, "replica", "mp"),
        P(None, "replica", "mp"),
        P("replica", "mp"),
        P("replica", "mp"),
        P("replica", "mp"),
        P("replica"),
    )
    return jax.shard_map(
        shards,
        mesh=mesh,
        in_specs=placed,
        out_specs=(P(None, "replica", "mp"), P(None, "replica", "mp"), P("replica", None, "mp")),
        check_vma=False,
    )
```

time: 233 us -> 117 us (0.50)
  Pallas kernels: 0 us -> 108 us
  blocking collectives: 107 us -> 0 us
  waiting for transfers between devices: 68.2 us -> 0 us
  other arithmetic: 15.8 us -> 0 us
  matrix products: 15 us -> 0 us
  between operations: 14.9 us -> 0.65 us
  local copies, waits for them, and re-layouts: 11.6 us -> 8.3 us
    pallas_call x0 -> x1, Pallas kernels: none -> 108 us  [shards(): pl.pallas_call(functools.partial(kernel, plan), out_shape=(jax.ShapeDtype...]
    all_to_all x1 -> x0, blocking collectives: 76.5 us -> none  [shards(): lax.all_to_all(pseudo_grad, 'replica', split_axis=2, concat_axis=0, tiled...]
    psum x1 -> x0, waiting for transfers between devices: 43.8 us -> none  [shards(): lax.psum(partial_branch.astype(jnp.bfloat16), 'mp').astype(jnp.float32)]
    all_gather x1 -> x0, waiting for transfers between devices: 24.4 us -> none  [shards(): lax.all_gather(new_outer.astype(jnp.bfloat16), 'replica', axis=1, tiled=T...]
    all_gather x1 -> x0, blocking collectives: 19.8 us -> none  [shards(): full_x = lax.all_gather(acts, 'mp', axis=1, tiled=True)]
    dot_general x7 -> x0, matrix products: 15 us -> none  [the longest x1 5.07 us: shards(): lax.dot_general(normed, pulled.reshape(count, cols), (((0,), (0,)), ((),...]
    psum x1 -> x0, blocking collectives: 10.6 us -> none  [shards(): squares = lax.psum(jnp.sum(grad * grad), 'mp')]
    reduce_sum x2 -> x0, other arithmetic: 6.5 us -> none  [the longest x1 6.26 us: shards(): summed = jnp.sum(blocks.astype(jnp.float32), axis=0)]
  transfers between devices with their start and end apart: 2 -> 0, of which waited for: 2 -> 0; matrix products, arithmetic and copies ran while one was open for 0% -> 0% of each run, Pallas kernels for 0% -> 0%
where the time goes in v1:
time: 117 us
  Pallas kernels  108 us (92%)
  local copies, waits for them, and re-layouts  8.3 us (7%)
    pallas_call x1, Pallas kernels, shards(): pl.pallas_call(functools.partial(kernel, plan), out_shape=(jax.ShapeDtype...  108 us
    unnamed x7, local copies, waits for them, and re-layouts  6.91 us

profile of v1, /device:TPU:0, one launch (start us, length us, event | category | flops | bytes accessed | tf_op | source)
XLA Modules:
  0.0 117.1 jit_solution(17033871791201367613)
XLA Ops:
  0.6 1.4 %copy.10.dcol = s32[128,1]{1,0:T(8,128)} copy(s32[128,1]{0,1:T(1,128)} %bitcast.4) | data formatting | bytes 1024 | tf_op jit(solution)/shard_map/reshape | solution.py:478
  2.0 108.2 %shard_map.94 = (f32[2,384,512]{2,1,0:T(8,128)}, f32[2,384,512]{2,1,0:T(8,128)}, bf16[1,3072,512]{2,1,0:T(8,128)(2,1)}) custom-call(bf16[2,4,2,384,512]{4,3,2,1,0:T(8,128)(2,1)} %bitcast.3, f32[2,384,512]{2,1,0:T(8,128)} %op.1, f32[2,384,512]{2,1,0:T(8,128)} %mo.1, bf16[128,768]{1,0:T(8,128)(2,1)} %acts.1, bf16[128,512]{1,0:T(8,128)(2,1)} %qs.1, ...), custom_call_target="tpu_custom_call" | custom-call | tf_op jit(solution)/shard_map/pallas_call | solution.py:466
  110.2 0.0 copy-start.1
  110.2 2.8 %copy.14 = f32[2,384,512]{2,1,0:T(8,128)} copy(f32[2,384,512]{2,1,0:T(8,128)} %get-tuple-element.6) | data formatting | bytes 3145728
  113.0 0.0 copy-done.1
  113.0 0.0 copy-start
  113.0 1.1 copy.15
  114.1 1.3 %copy-done = bf16[1,3072,512]{2,1,0:T(8,128)(2,1)S(1)} copy-done((bf16[1,3072,512]{2,1,0:T(8,128)(2,1)S(1)}, bf16[1,3072,512]{2,1,0:T(8,128)(2,1)}, u32[]{:S(2)}) %copy-start) | copy-done | bytes 3145752
  115.4 1.7 %copy.16 = bf16[1,3072,512]{2,1,0:T(8,128)(2,1)} copy(bf16[1,3072,512]{2,1,0:T(8,128)(2,1)S(1)} %copy-done) | data formatting | bytes 6291456
Async XLA Ops:
  110.2 2.8 %copy-start.1 = (f32[2,384,512]{2,1,0:T(8,128)S(1)}, f32[2,384,512]{2,1,0:T(8,128)}, u32[]{:S(2)}) copy-start(f32[2,384,512]{2,1,0:T(8,128)} %get-tuple-element.7) | copy-start | bytes 4718596
  113.0 2.5 %copy-start = (bf16[1,3072,512]{2,1,0:T(8,128)(2,1)S(1)}, bf16[1,3072,512]{2,1,0:T(8,128)(2,1)}, u32[]{:S(2)}) copy-start(bf16[1,3072,512]{2,1,0:T(8,128)(2,1)} %get-tuple-element.8) | copy-start | bytes 9437188

commit v2 on v1

--- a/solution.py
+++ b/solution.py
@@ -53,10 +53,10 @@
         self.order = [[0] + list(range(1, k)) if h % 2 == 0 else [0] + list(range(k - 1, 0, -1)) for _, h in self.streams]
 
 
-def kernel(pl_, pg, op, mo, acts, qs, ks, dcol, drow, out_o, out_m, out_l,
-           mine, r0, snds, recvs, opv, mov, nov, nmv, w, xg, xd, nrm, nrt, probs,
-           pb, zr, zs, db, lov, sq, sqr,
-           mine_sem, in_sem, r0_sem, rs_sem, ag_send, ag_recv, x_sem, z_send, z_recv, g_send, g_recv, q_sem, out_sem):
+def kernel(pl_, pg, op, mo, acts_h, qs_h, ks_h, drow, out_o, out_m, w0o, nro, dvo, faco,
+           mine, r0, snds, recvs, opv, mov, w, qs, ks, xg, xd, nrm, probs,
+           pb, zr, zs, db, sq, sqr,
+           mine_sem, in_sem, r0_sem, rs_sem, ag_send_sem, ag_recv, x_sem, z_send, z_recv, g_send, g_recv, q_sem):
     n, groups, R, cols, count, width = pl_.n, pl_.groups, pl_.rows, pl_.cols, pl_.count, pl_.width
     k, kz, chunk = pl_.k, pl_.kz, pl_.chunk
     me = lax.axis_index("replica")
@@ -76,19 +76,23 @@
     def hs(h):
         return pl.ds(h * HD, HD)
 
-    mine_cp = []
-    for s, (m, h) in enumerate(S):
-        c = pltpu.make_async_copy(pg.at[m, :, b0, :, hs(h)], mine.at[s], mine_sem.at[s])
-        c.start()
-        mine_cp.append(c)
-    op_cp = pltpu.make_async_copy(op, opv, in_sem.at[0])
-    mo_cp = pltpu.make_async_copy(mo, mov, in_sem.at[1])
-
     bar = pltpu.get_barrier_semaphore()
     for j in range(k):
         pl.semaphore_signal(bar, inc=1, device_id=rep(1 << j), device_id_type=MESH)
     for mask in range(1, groups):
         pl.semaphore_signal(bar, inc=1, device_id=zdev(mask), device_id_type=MESH)
+    mine_cp = []
+    for s, (m, h) in enumerate(S):
+        c = pltpu.make_async_copy(pg.at[m, :, b0, :, hs(h)], mine.at[s], mine_sem.at[s])
+        c.start()
+        mine_cp.append(c)
+    op_cp = pltpu.make_async_copy(op, opv, in_sem.at[0])
+    mo_cp = pltpu.make_async_copy(mo, mov, in_sem.at[1])
+    act_cp = [pltpu.make_async_copy(src, dst, in_sem.at[2 + i])
+              for i, (src, dst) in enumerate(((qs_h, qs), (ks_h, ks), (acts_h, xg.at[0])))]
+    for c in act_cp:
+        c.start()
+
     pl.semaphore_wait(bar, k + groups - 1)
 
     r0_cp = []
@@ -101,7 +105,7 @@
     x_cp = []
     for mask in range(1, groups):
         c = pltpu.make_async_remote_copy(
-            src_ref=acts, dst_ref=xg.at[mask], send_sem=x_sem.at[0, mask], recv_sem=x_sem.at[1, mask],
+            src_ref=acts_h, dst_ref=xg.at[mask], send_sem=x_sem.at[0, mask], recv_sem=x_sem.at[1, mask],
             device_id=zdev(mask), device_id_type=MESH)
         c.start()
         x_cp.append(c)
@@ -163,23 +167,27 @@
             masks = masks + [x ^ (1 << b) for x in masks]
         return masks
 
-    def ag_send_block(s, mask, first):
+    def ag_send(s, mask, e):
         m, h = S[s]
-        for e in range(first, k):
-            i = held(s, e).index(mask)
-            ref = w.at[m, flip(me, mask, k), :, hs(h)]
-            cp = pltpu.make_async_remote_copy(
-                src_ref=ref, dst_ref=ref, send_sem=ag_send.at[s, (1 << e) + i], recv_sem=ag_recv.at[s, (1 << e) + i],
-                device_id=rep(1 << order[s][k - 1 - e]), device_id_type=MESH)
-            cp.start()
-            ag[s, e, i] = cp
+        i = held(s, e).index(mask)
+        ref = w.at[m, flip(me, mask, k), :, hs(h)]
+        cp = pltpu.make_async_remote_copy(
+            src_ref=ref, dst_ref=ref, send_sem=ag_send_sem.at[s, (1 << e) + i], recv_sem=ag_recv.at[s, (1 << e) + i],
+            device_id=rep(1 << order[s][k - 1 - e]), device_id_type=MESH)
+        cp.start()
+        ag[s, e, i] = cp
+
+    def ag_send_own(group):
+        for e in range(k):
+            for s in group:
+                ag_send(s, 0, e)
 
     def ag_wait_block(s, e, i):
         m, h = S[s]
         mask = held(s, e)[i] ^ (1 << order[s][k - 1 - e])
         ref = w.at[m, flip(me, mask, k), :, hs(h)]
         pltpu.make_async_remote_copy(
-            src_ref=ref, dst_ref=ref, send_sem=ag_send.at[s, (1 << e) + i], recv_sem=ag_recv.at[s, (1 << e) + i],
+            src_ref=ref, dst_ref=ref, send_sem=ag_send_sem.at[s, (1 << e) + i], recv_sem=ag_recv.at[s, (1 << e) + i],
             device_id=rep(1 << order[s][k - 1 - e]), device_id_type=MESH).wait_recv()
         return mask
 
@@ -197,8 +205,8 @@
             delta = block_sum(s, last, 0)(rs) / n
             mn = outer_beta * mov[m, rs, hs(h)] + delta
             on = opv[m, rs, hs(h)] - outer_rate * (delta + outer_beta * mn)
-            nmv[m, rs, hs(h)] = mn
-            nov[m, rs, hs(h)] = on
+            out_m[m, rs, hs(h)] = mn
+            out_o[m, rs, hs(h)] = on
             w[m, me, rs, hs(h)] = on.astype(BF16)
             return 0
         lax.fori_loop(0, R // T, body, 0)
@@ -206,8 +214,11 @@
     of = [s for s, (m, h) in enumerate(S) if m == 0]
     oo = [s for s, (m, h) in enumerate(S) if m == 1]
 
+    for c in act_cp:
+        c.wait()
     allowed = lax.broadcasted_iota(jnp.int32, (count, count), 0) >= lax.broadcasted_iota(jnp.int32, (count, count), 1)
-    allowed = allowed & (dcol[...] == drow[...])
+    docs = jnp.broadcast_to(drow[...], (count, count))
+    allowed = allowed & (docs.T == docs)
     for h in range(pl_.heads):
         sc = dot(qs[:, hs(h)], ks[:, hs(h)], 1, 1) * HD ** (-0.5)
         sc = jnp.where(allowed, sc, -1e30)
@@ -218,7 +229,6 @@
         if k > 1:
             rs_stage(s, 1)
 
-    xg[0] = acts[...]
     for c in x_cp:
         c.wait_recv()
     ssum = jnp.zeros((count, 1), F32)
@@ -231,7 +241,7 @@
         xf = xg[g].astype(F32)
         nb = (xf * inv).astype(BF16)
         nrm[g] = nb
-        nrt[g] = nb.astype(F32).T.astype(BF16)
+        nro[flip(mz, g, kz)] = nb.astype(F32).T.astype(BF16)
         gram = gram + dot(nb, nb, 1, 1)
         xd[g] = xf - pltpu.roll(xf, count - 1, 0)
 
@@ -243,29 +253,26 @@
     mo_cp.wait()
     for s in of:
         update(s)
-        ag_send_block(s, 0, 0)
+    ag_send_own(of)
     for s in oo:
         update(s)
-    out_cp = [pltpu.make_async_copy(nov, out_o, out_sem.at[0]), pltpu.make_async_copy(nmv, out_m, out_sem.at[1])]
-    for c in out_cp:
-        c.start()
-
-    def forward(group, e):
+
+    def arrive(group, e, i):
+        masks = [ag_wait_block(s, e, i) for s in group]
+        for ee in range(e + 1, k):
+            for s, mask in zip(group, masks):
+                ag_send(s, mask, ee)
+        return masks
+
+    for e in range(k - 1):
         for i in range(1 << e):
-            for s in group:
-                mask = ag_wait_block(s, e, i)
-                if e + 1 < k:
-                    ag_send_block(s, mask, e + 1)
-
-    for e in range(k - 1):
-        forward(of, e)
+            arrive(of, e, i)
         if e == 0:
-            for s in oo:
-                ag_send_block(s, 0, 0)
+            ag_send_own(oo)
     if k == 1:
-        for s in oo:
-            ag_send_block(s, 0, 0)
-    forward(of, k - 1)
+        ag_send_own(oo)
+    for i in range(1 << (k - 1)):
+        arrive(of, k - 1, i)
 
     def wrows(m, g):
         part = w[m, pl.ds(pl.multiple_of(g * (n // groups), n // groups), n // groups)]
@@ -374,25 +381,49 @@
         elif j <= 2 * kz:
             z_forward(c, j - kz - 1)
 
-    ready = set([0 if False else None])
-    arrived = {s: 0 for s in oo}
+    last_step = 2 * kz + 1
+    have = {s: {0} for s in oo}
+    stage = {}
+
+    def start_ready():
+        for c in range(groups):
+            if c in stage:
+                continue
+            evens = [x for x in range(c * per, (c + 1) * per) if x % 2 == 0]
+            if all(x in have[s] for s in oo for x in evens):
+                for s in oo:
+                    for x in evens:
+                        ag_wait_block(s, k - 1, held(s, k - 1).index(x))
+                z_step(c, 0)
+                stage[c] = 1
+
+    def advance(c):
+        if c in stage and stage[c] < last_step:
+            z_step(c, stage[c])
+            stage[c] += 1
+
+    start_ready()
     for e in range(k - 1):
-        forward(oo, e)
-    forward(oo, k - 1)
-
-    steps = 2 * kz + 1
-    for wave in range(groups + steps - 1):
-        for c in range(groups):
-            j = wave - c
-            if 0 <= j < steps:
-                z_step(c, j)
+        for i in range(1 << e):
+            running = [c for c in stage]
+            for s, mask in zip(oo, arrive(oo, e, i)):
+                have[s].add(mask)
+            start_ready()
+            for c in running:
+                advance(c)
+    w0o[...] = w[0].reshape(width, cols)
+    while any(stage[c] < last_step - 1 for c in stage):
+        advance(min(stage, key=lambda c: (stage[c], c)))
 
     dctx = jnp.zeros((count, cols), F32)
     for c in range(groups):
+        advance(c)
         dctx = dctx + dot(db[c], wrows(1, gidx(c)), 1, 0)
     dctx = (dctx * scale).astype(BF16)
     dv = jnp.concatenate(
         [dot(probs[h], dctx[:, h * HD:(h + 1) * HD], 0, 0).astype(BF16) for h in range(pl_.heads)], axis=1)
+
+    dvo[...] = dv
 
     part = jnp.sum(gram * dot(dv, dv, 1, 1), axis=0, keepdims=True) / width
     sq[...] = jnp.broadcast_to(part, (8, count))
@@ -410,19 +441,25 @@
     total = jnp.sum(tot[0:1, :], axis=1, keepdims=True)
     total = jnp.maximum(total, 0.0) / (width * cols * groups)
     fac = (inner_rate * width ** (-0.5)) * lax.rsqrt(total + norm_eps)
-    for g in range(groups):
-        z = flip(mz, g, kz)
-        grad = dot(nrt[g], dv, 1, 0)
-        rows = pl.ds(pl.multiple_of(z * chunk, chunk), chunk)
-        lov[rows, :] = (wrows(0, z).astype(F32) - grad * fac).astype(BF16)
-        c = pltpu.make_async_copy(lov.at[rows], out_l.at[0, rows], out_sem.at[2 + g])
-        c.start()
-        out_cp.append(c)
-
-    for c in out_cp:
-        c.wait()
+    faco[...] = jnp.broadcast_to(fac, faco.shape)
+
     for c in r0_cp + x_cp + qcp + list(rs_cp.values()) + list(ag.values()) + list(zcp.values()) + list(gcp.values()):
         c.wait_send()
+
+
+def finish(pl_, no, nm, w0, nrt, dv, fac, out_o, out_m, out_l, lov, out_sem):
+    copies = [pltpu.make_async_copy(no, out_o, out_sem.at[0]), pltpu.make_async_copy(nm, out_m, out_sem.at[1])]
+    for c in copies:
+        c.start()
+    for g in range(pl_.groups):
+        rows = slice(g * pl_.chunk, (g + 1) * pl_.chunk)
+        grad = dot(nrt[g], dv[...], 1, 0)
+        lov[rows, :] = (w0[rows, :].astype(F32) - grad * fac[0:1, :]).astype(BF16)
+        c = pltpu.make_async_copy(lov.at[rows], out_l.at[0, rows], out_sem.at[2 + g])
+        c.start()
+        copies.append(c)
+    for c in copies:
+        c.wait()
 
 
 def shards(pseudo_grad, outer_params, momentum, acts, queries, keys, doc_ids):
@@ -435,7 +472,7 @@
     k, kz, ns, chunk = plan.k, plan.kz, len(plan.streams), plan.chunk
     half = n // 2
     pg = pseudo_grad.reshape(mats, half, 2, rows, cols)
-    vm, anym = pl.BlockSpec(memory_space=pltpu.VMEM), pl.BlockSpec(memory_space=pl.ANY)
+    vm = pl.BlockSpec(memory_space=pltpu.VMEM)
     dma = pltpu.SemaphoreType.DMA
     scratch = [
         pltpu.VMEM((ns, half, rows, HD), BF16),
@@ -444,38 +481,53 @@
         [pltpu.VMEM((ns, half >> t, rows, HD), BF16) for t in range(1, k)],
         pltpu.VMEM((mats, rows, cols), F32),
         pltpu.VMEM((mats, rows, cols), F32),
-        pltpu.VMEM((mats, rows, cols), F32),
-        pltpu.VMEM((mats, rows, cols), F32),
         pltpu.VMEM((mats, n, rows, cols), BF16),
+        pltpu.VMEM((count, cols), BF16),
+        pltpu.VMEM((count, cols), BF16),
         pltpu.VMEM((groups, count, chunk), BF16),
         pltpu.VMEM((groups, count, chunk), F32),
         pltpu.VMEM((groups, count, chunk), BF16),
-        pltpu.VMEM((groups, chunk, count), BF16),
         pltpu.VMEM((plan.heads, count, count), BF16),
         pltpu.VMEM((groups, count, chunk), BF16),
         [pltpu.VMEM((groups, count >> (t + 1), chunk), BF16) for t in range(kz)],
         [pltpu.VMEM((groups, count >> (t + 1), chunk), BF16) for t in range(1, kz)],
         pltpu.VMEM((groups, count, chunk), BF16),
-        pltpu.VMEM((width, cols), BF16),
         pltpu.VMEM((8, count), F32),
         pltpu.VMEM((groups, 8, count), F32),
-        dma((ns,)), dma((2,)), dma((2, ns)), dma((2, k, ns)), dma((ns, n)), dma((ns, n)),
+        dma((ns,)), dma((5,)), dma((2, ns)), dma((2, k, ns)), dma((ns, n)), dma((ns, n)),
         dma((2, groups)), dma((kz, groups)), dma((kz, groups)), dma((groups, groups)), dma((groups, groups)),
-        dma((2, groups)), dma((2 + groups,)),
+        dma((2, groups)),
     ]
+    hbm = pl.BlockSpec(memory_space=pltpu.HBM)
+    new_outer, new_momentum, w0, nrt, dv, fac = pl.pallas_call(
+        functools.partial(kernel, plan),
+        out_shape=(
+            jax.ShapeDtypeStruct(outer_params.shape, F32),
+            jax.ShapeDtypeStruct(momentum.shape, F32),
+            jax.ShapeDtypeStruct((width, cols), BF16),
+            jax.ShapeDtypeStruct((groups, chunk, count), BF16),
+            jax.ShapeDtypeStruct((count, cols), BF16),
+            jax.ShapeDtypeStruct((8, cols), F32),
+        ),
+        in_specs=[hbm] * 6 + [vm],
+        out_specs=(vm,) * 6,
+        scratch_shapes=scratch,
+        compiler_params=pltpu.CompilerParams(
+            collective_id=0, has_side_effects=True, vmem_limit_bytes=36 * 1024 * 1024),
+    )(*[pltpu.with_memory_space_constraint(t, pltpu.HBM) for t in (pg, outer_params, momentum, acts, queries, keys)],
+      doc_ids.reshape(1, count))
     return pl.pallas_call(
-        functools.partial(kernel, plan),
+        functools.partial(finish, plan),
         out_shape=(
             jax.ShapeDtypeStruct(outer_params.shape, F32),
             jax.ShapeDtypeStruct(momentum.shape, F32),
             jax.ShapeDtypeStruct((1, width, cols), BF16),
         ),
-        in_specs=[anym, anym, anym, vm, vm, vm, vm, vm],
-        out_specs=(anym, anym, anym),
-        scratch_shapes=scratch,
-        compiler_params=pltpu.CompilerParams(
-            collective_id=0, has_side_effects=True, vmem_limit_bytes=62 * 1024 * 1024),
-    )(pg, outer_params, momentum, acts, queries, keys, doc_ids.reshape(count, 1), doc_ids.reshape(1, count))
+        in_specs=[vm] * 6,
+        out_specs=(hbm,) * 3,
+        scratch_shapes=[pltpu.VMEM((width, cols), BF16), dma((2 + groups,))],
+        compiler_params=pltpu.CompilerParams(vmem_limit_bytes=16 * 1024 * 1024),
+    )(new_outer, new_momentum, w0, nrt, dv, fac)
 
 
 def solution(mesh):

time: 117 us -> 96 us (0.82)
  Pallas kernels: 108 us -> 94.5 us
  local copies, waits for them, and re-layouts: 8.3 us -> 0.65 us
    pallas_call x1, Pallas kernels: 108 us -> 91.8 us  [shards(): pl.pallas_call(functools.partial(kernel, plan), out_shape=(jax.ShapeDtype...]
    unnamed x7 -> x2, local copies, waits for them, and re-layouts: 6.91 us -> 0.65 us
    pallas_call x0 -> x1, Pallas kernels: none -> 2.73 us  [shards(): pl.pallas_call(functools.partial(finish, plan), out_shape=(jax.ShapeDtype...]
    reshape x1 -> x0, local copies, waits for them, and re-layouts: 1.39 us -> none  [shards(): doc_ids.reshape(count, 1)]
where the time goes in v2:
time: 96 us; the launch traced here: 95.8 us
  Pallas kernels  94.5 us (98%)
    pallas_call x1, Pallas kernels, shards(): pl.pallas_call(functools.partial(kernel, plan), out_shape=(jax.ShapeDtype...  91.8 us
    pallas_call x1, Pallas kernels, shards(): pl.pallas_call(functools.partial(finish, plan), out_shape=(jax.ShapeDtype...  2.73 us

profile of v2, /device:TPU:0, one launch (start us, length us, event | category | flops | bytes accessed | tf_op | source)
XLA Modules:
  0.0 95.8 jit_solution(4487697737911785610)
XLA Ops:
  0.6 0.0 copy-start
  0.6 0.6 copy-done
  1.3 91.8 %shard_map.94 = (f32[2,384,512]{2,1,0:T(8,128)S(1)}, f32[2,384,512]{2,1,0:T(8,128)S(1)}, bf16[3072,512]{1,0:T(8,128)(2,1)S(1)}, bf16[4,768,128]{2,1,0:T(8,128)(2...) custom-call(bf16[2,4,2,384,512]{4,3,2,1,0:T(8,128)(2,1)} %bitcast.3, f32[2,384,512]{2,1,0:T(8,128)} %op.1, ...), custom_call_target="tpu_custom_call" | custom-call | tf_op jit(solution)/shard_map/pallas_call | solution.py:502
  93.1 2.7 %shard_map.95 = (f32[2,384,512]{2,1,0:T(8,128)}, f32[2,384,512]{2,1,0:T(8,128)}, bf16[1,3072,512]{2,1,0:T(8,128)(2,1)}) custom-call(f32[2,384,512]{2,1,0:T(8,128)S(1)} %get-tuple-element.9.no, f32[2,384,512]{2,1,0:T(8,128)S(1)} %get-tuple-element.10.nm, bf16[3072,512]{1,0:T(8,128)(2,1)S(1)} %get-tuple-element.11.w0, ...), custom_call_target="tpu_custom_call" | custom-call | tf_op jit(solution)/shard_map/pallas_call | solution.py:519
Async XLA Ops:
  0.6 0.7 copy-start

commit v3 on v2

--- a/solution.py
+++ b/solution.py
@@ -48,15 +48,17 @@
         self.kz = groups.bit_length() - 1
         self.heads = cols // HD
         self.chunk = width // groups
+        self.parts = 2 * groups if n % (2 * groups) == 0 and width // (2 * groups) % 128 == 0 else groups
+        self.zc = width // self.parts
         self.streams = [(m, h) for m in range(2) for h in range(self.heads)]
         k = self.k
         self.order = [[0] + list(range(1, k)) if h % 2 == 0 else [0] + list(range(k - 1, 0, -1)) for _, h in self.streams]
 
 
-def kernel(pl_, pg, op, mo, acts_h, qs_h, ks_h, drow, out_o, out_m, w0o, nro, dvo, faco,
-           mine, r0, snds, recvs, opv, mov, w, qs, ks, xg, xd, nrm, probs,
+def kernel(pl_, pg, op, mo, acts_h, qs_h, ks_h, docs_h, out_o, out_m, w0o, nro, dvo, faco,
+           mine, r0, snds, recvs, opv, mov, w, qs, ks, drow, xg, xd, nrm, probs,
            pb, zr, zs, db, sq, sqr,
-           mine_sem, in_sem, r0_sem, rs_sem, ag_send_sem, ag_recv, x_sem, z_send, z_recv, g_send, g_recv, q_sem):
+           mine_sem, in_sem, r0_sem, r1_sem, rs_sem, ag_send_sem, ag_recv, x_sem, z_send, z_recv, g_send, g_recv, q_sem):
     n, groups, R, cols, count, width = pl_.n, pl_.groups, pl_.rows, pl_.cols, pl_.count, pl_.width
     k, kz, chunk = pl_.k, pl_.kz, pl_.chunk
     me = lax.axis_index("replica")
@@ -89,7 +91,7 @@
     op_cp = pltpu.make_async_copy(op, opv, in_sem.at[0])
     mo_cp = pltpu.make_async_copy(mo, mov, in_sem.at[1])
     act_cp = [pltpu.make_async_copy(src, dst, in_sem.at[2 + i])
-              for i, (src, dst) in enumerate(((qs_h, qs), (ks_h, ks), (acts_h, xg.at[0])))]
+              for i, (src, dst) in enumerate(((qs_h, qs), (ks_h, ks), (docs_h, drow), (acts_h, xg.at[0])))]
     for c in act_cp:
         c.start()
 
@@ -136,12 +138,38 @@
 
     rs_cp = {}
 
-    def rs_stage(s, t):
-        if t == 1:
+    def rs_wait(s, t):
+        if t == 0:
             mine_cp[s].wait()
             r0_cp[s].wait_recv()
+        elif t == 1:
+            for u in range(n // 4):
+                rs_cp[s, 1, u].wait_recv()
         else:
-            rs_cp[s, t - 1].wait_recv()
+            rs_cp[s, t].wait_recv()
+
+    def rs_first(group):
+        for u in range(n // 4):
+            for s in group:
+                if u == 0:
+                    rs_wait(s, 0)
+                other = 1 - bit_of(me, order[s][1])
+                rows_at = block_sum(s, 0, level_up(s, 1, u, other))
+
+                def body(i, _, s=s, u=u, rows_at=rows_at):
+                    rs = pl.ds(pl.multiple_of(i * T, T), T)
+                    snds[0][s, u, rs, :] = rows_at(rs).astype(BF16)
+                    return 0
+                lax.fori_loop(0, R // T, body, 0)
+                cp = pltpu.make_async_remote_copy(
+                    src_ref=snds[0].at[s, u], dst_ref=recvs[0].at[s, u],
+                    send_sem=r1_sem.at[0, s, u], recv_sem=r1_sem.at[1, s, u],
+                    device_id=rep(1 << order[s][1]), device_id_type=MESH)
+                cp.start()
+                rs_cp[s, 1, u] = cp
+
+    def rs_stage(s, t):
+        rs_wait(s, t - 1)
         c = (n // 2) >> t
         other = 1 - bit_of(me, order[s][t])
 
@@ -194,11 +222,7 @@
     def update(s):
         m, h = S[s]
         last = k - 1
-        if last == 0:
-            mine_cp[s].wait()
-            r0_cp[s].wait_recv()
-        else:
-            rs_cp[s, last].wait_recv()
+        rs_wait(s, last)
 
         def body(i, _):
             rs = pl.ds(pl.multiple_of(i * T, T), T)
@@ -225,9 +249,9 @@
         ex = jnp.exp(sc - jnp.max(sc, axis=1, keepdims=True))
         probs[h] = (ex / jnp.sum(ex, axis=1, keepdims=True)).astype(BF16)
 
-    for s in of + oo:
-        if k > 1:
-            rs_stage(s, 1)
+    if k > 1:
+        rs_first(of)
+        rs_first(oo)
 
     for c in x_cp:
         c.wait_recv()
@@ -286,12 +310,15 @@
         [dot(probs[h], vals[:, h * HD:(h + 1) * HD], 1, 0).astype(BF16) for h in range(pl_.heads)], axis=1)
 
     scale = (cols * groups) ** (-0.5)
-    per = n // groups
-    kg = kz
+    NC, zc = pl_.parts, pl_.zc
+    per = n // NC
     gme = me // per
 
     def gidx(c):
-        return flip(gme, c, kg)
+        return flip(gme, c, NC.bit_length() - 1)
+
+    def zrows(c):
+        return w[1, pl.ds(pl.multiple_of(gidx(c) * per, per), per)].reshape(zc, cols)
 
     size = [count >> t for t in range(kz + 1)]
     start = [0]
@@ -307,7 +334,7 @@
 
     def z_reduce(c, t):
         if t == 0:
-            pb[c] = (dot(ctx, wrows(1, gidx(c)), 1, 1) * scale).astype(BF16)
+            pb[c] = (dot(ctx, zrows(c), 1, 1) * scale).astype(BF16)
         else:
             zcp[c, t - 1].wait_recv()
         num = size[t + 1]
@@ -355,8 +382,9 @@
         zcp[c, kz - 1].wait_recv()
         lo, num = start[kz], size[kz]
         tot = z_rows(c, kz, lo, num)
-        xz = flip(gidx(c), 0, kz)
-        tot = tot + xd[xmask(xz), pl.ds(pl.multiple_of(lo, num), num), :]
+        each = NC // groups
+        lanes = pl.ds(pl.multiple_of((gidx(c) % each) * zc, zc), zc)
+        tot = tot + xd[xmask(gidx(c) // each), pl.ds(pl.multiple_of(lo, num), num), lanes]
         db[c, pl.ds(pl.multiple_of(lo, num), num), :] = tot.astype(BF16)
         z_send_block(c, 0, 0)
 
@@ -385,15 +413,16 @@
     have = {s: {0} for s in oo}
     stage = {}
 
-    def start_ready():
-        for c in range(groups):
-            if c in stage:
+    def start_ready(with_odd):
+        for c in range(NC):
+            masks = range(c * per, (c + 1) * per)
+            odds = [x for x in masks if x % 2 == 1]
+            if c in stage or (odds and not with_odd):
                 continue
-            evens = [x for x in range(c * per, (c + 1) * per) if x % 2 == 0]
-            if all(x in have[s] for s in oo for x in evens):
+            if all(x - x % 2 in have[s] for s in oo for x in masks):
                 for s in oo:
-                    for x in evens:
-                        ag_wait_block(s, k - 1, held(s, k - 1).index(x))
+                    for x in odds:
+                        ag_wait_block(s, k - 1, held(s, k - 1).index(x - 1))
                 z_step(c, 0)
                 stage[c] = 1
 
@@ -402,23 +431,30 @@
             z_step(c, stage[c])
             stage[c] += 1
 
-    start_ready()
+    start_ready(False)
+    start_ready(True)
+    late = []
     for e in range(k - 1):
         for i in range(1 << e):
-            running = [c for c in stage]
+            running = [c for c in stage if stage[c] < last_step - 1 and c not in late]
             for s, mask in zip(oo, arrive(oo, e, i)):
                 have[s].add(mask)
-            start_ready()
+            start_ready(False)
             for c in running:
                 advance(c)
+            started = list(stage)
+            start_ready(True)
+            for c in late:
+                advance(c)
+            late = [c for c in stage if c not in started]
     w0o[...] = w[0].reshape(width, cols)
     while any(stage[c] < last_step - 1 for c in stage):
         advance(min(stage, key=lambda c: (stage[c], c)))
 
     dctx = jnp.zeros((count, cols), F32)
-    for c in range(groups):
+    for c in range(NC):
         advance(c)
-        dctx = dctx + dot(db[c], wrows(1, gidx(c)), 1, 0)
+        dctx = dctx + dot(db[c], zrows(c), 1, 0)
     dctx = (dctx * scale).astype(BF16)
     dv = jnp.concatenate(
         [dot(probs[h], dctx[:, h * HD:(h + 1) * HD], 0, 0).astype(BF16) for h in range(pl_.heads)], axis=1)
@@ -434,6 +470,8 @@
             device_id=zdev(mask), device_id_type=MESH)
         c.start()
         qcp.append(c)
+    for c in r0_cp + x_cp + list(rs_cp.values()) + list(ag.values()) + list(zcp.values()) + list(gcp.values()):
+        c.wait_send()
     tot = sq[...]
     for i, c in enumerate(qcp):
         c.wait_recv()
@@ -443,7 +481,7 @@
     fac = (inner_rate * width ** (-0.5)) * lax.rsqrt(total + norm_eps)
     faco[...] = jnp.broadcast_to(fac, faco.shape)
 
-    for c in r0_cp + x_cp + qcp + list(rs_cp.values()) + list(ag.values()) + list(zcp.values()) + list(gcp.values()):
+    for c in qcp:
         c.wait_send()
 
 
@@ -470,6 +508,7 @@
     count = acts.shape[0]
     plan = Plan(n, groups, rows, cols, count, width)
     k, kz, ns, chunk = plan.k, plan.kz, len(plan.streams), plan.chunk
+    parts, zc = plan.parts, plan.zc
     half = n // 2
     pg = pseudo_grad.reshape(mats, half, 2, rows, cols)
     vm = pl.BlockSpec(memory_space=pltpu.VMEM)
@@ -484,18 +523,19 @@
         pltpu.VMEM((mats, n, rows, cols), BF16),
         pltpu.VMEM((count, cols), BF16),
         pltpu.VMEM((count, cols), BF16),
+        pltpu.VMEM((1, count), jnp.int32),
         pltpu.VMEM((groups, count, chunk), BF16),
         pltpu.VMEM((groups, count, chunk), F32),
         pltpu.VMEM((groups, count, chunk), BF16),
         pltpu.VMEM((plan.heads, count, count), BF16),
-        pltpu.VMEM((groups, count, chunk), BF16),
-        [pltpu.VMEM((groups, count >> (t + 1), chunk), BF16) for t in range(kz)],
-        [pltpu.VMEM((groups, count >> (t + 1), chunk), BF16) for t in range(1, kz)],
-        pltpu.VMEM((groups, count, chunk), BF16),
+        pltpu.VMEM((parts, count, zc), BF16),
+        [pltpu.VMEM((parts, count >> (t + 1), zc), BF16) for t in range(kz)],
+        [pltpu.VMEM((parts, count >> (t + 1), zc), BF16) for t in range(1, kz)],
+        pltpu.VMEM((parts, count, zc), BF16),
         pltpu.VMEM((8, count), F32),
         pltpu.VMEM((groups, 8, count), F32),
-        dma((ns,)), dma((5,)), dma((2, ns)), dma((2, k, ns)), dma((ns, n)), dma((ns, n)),
-        dma((2, groups)), dma((kz, groups)), dma((kz, groups)), dma((groups, groups)), dma((groups, groups)),
+        dma((ns,)), dma((6,)), dma((2, ns)), dma((2, ns, max(n // 4, 1))), dma((2, k, ns)), dma((ns, n)), dma((ns, n)),
+        dma((2, groups)), dma((kz, parts)), dma((kz, parts)), dma((parts, groups)), dma((parts, groups)),
         dma((2, groups)),
     ]
     hbm = pl.BlockSpec(memory_space=pltpu.HBM)
@@ -509,13 +549,13 @@
             jax.ShapeDtypeStruct((count, cols), BF16),
             jax.ShapeDtypeStruct((8, cols), F32),
         ),
-        in_specs=[hbm] * 6 + [vm],
+        in_specs=[hbm] * 7,
         out_specs=(vm,) * 6,
         scratch_shapes=scratch,
         compiler_params=pltpu.CompilerParams(
             collective_id=0, has_side_effects=True, vmem_limit_bytes=36 * 1024 * 1024),
-    )(*[pltpu.with_memory_space_constraint(t, pltpu.HBM) for t in (pg, outer_params, momentum, acts, queries, keys)],
-      doc_ids.reshape(1, count))
+    )(*[pltpu.with_memory_space_constraint(t, pltpu.HBM) for t in (
+        pg, outer_params, momentum, acts, queries, keys, doc_ids.reshape(1, count))])
     return pl.pallas_call(
         functools.partial(finish, plan),
         out_shape=(

time: 96 us -> 93.1 us (0.970)
  Pallas kernels: 94.5 us -> 92.4 us
    pallas_call x1, Pallas kernels: 91.8 us -> 89.6 us  [shards(): pl.pallas_call(functools.partial(kernel, plan), out_shape=(jax.ShapeDtype...]
where the time goes in v3:
time: 93.1 us; the launch traced here: 93 us
  Pallas kernels  92.4 us (99%)
    pallas_call x1, Pallas kernels, shards(): pl.pallas_call(functools.partial(kernel, plan), out_shape=(jax.ShapeDtype...  89.6 us
    pallas_call x1, Pallas kernels, shards(): pl.pallas_call(functools.partial(finish, plan), out_shape=(jax.ShapeDtype...  2.73 us

profile of v3, /device:TPU:0, one launch (start us, length us, event | category | flops | bytes accessed | tf_op | source)
XLA Modules:
  0.0 93.0 jit_solution(14792603136143246005)
XLA Ops:
  0.6 89.6 %shard_map.94 = (f32[2,384,512]{2,1,0:T(8,128)S(1)}, f32[2,384,512]{2,1,0:T(8,128)S(1)}, bf16[3072,512]{1,0:T(8,128)(2,1)S(1)}, bf16[4,768,128]{2,1,0:T(8,128)(2...) custom-call(bf16[2,4,2,384,512]{4,3,2,1,0:T(8,128)(2,1)} %bitcast.2, f32[2,384,512]{2,1,0:T(8,128)} %op.1, ...), custom_call_target="tpu_custom_call" | custom-call | tf_op jit(solution)/shard_map/pallas_call | solution.py:542
  90.3 2.7 %shard_map.95 = (f32[2,384,512]{2,1,0:T(8,128)}, f32[2,384,512]{2,1,0:T(8,128)}, bf16[1,3072,512]{2,1,0:T(8,128)(2,1)}) custom-call(f32[2,384,512]{2,1,0:T(8,128)S(1)} %get-tuple-element.9.no, f32[2,384,512]{2,1,0:T(8,128)S(1)} %get-tuple-element.10.nm, bf16[3072,512]{1,0:T(8,128)(2,1)S(1)} %get-tuple-element.11.w0, ...), custom_call_target="tpu_custom_call" | custom-call | tf_op jit(solution)/shard_map/pallas_call | solution.py:559

commit v4 on v3

--- a/solution.py
+++ b/solution.py
@@ -160,7 +160,7 @@
                     rs = pl.ds(pl.multiple_of(i * T, T), T)
                     snds[0][s, u, rs, :] = rows_at(rs).astype(BF16)
                     return 0
-                lax.fori_loop(0, R // T, body, 0)
+                lax.fori_loop(0, R // T, body, 0, unroll=True)
                 cp = pltpu.make_async_remote_copy(
                     src_ref=snds[0].at[s, u], dst_ref=recvs[0].at[s, u],
                     send_sem=r1_sem.at[0, s, u], recv_sem=r1_sem.at[1, s, u],
@@ -182,7 +182,7 @@
         lax.fori_loop(0, c * (R // T), body, 0)
         cp = pltpu.make_async_remote_copy(
             src_ref=snds[t - 1].at[s], dst_ref=recvs[t - 1].at[s],
-            send_sem=rs_sem.at[0, t - 1, s], recv_sem=rs_sem.at[1, t - 1, s],
+            send_sem=rs_sem.at[0, t - 2, s], recv_sem=rs_sem.at[1, t - 2, s],
             device_id=rep(1 << order[s][t]), device_id_type=MESH)
         cp.start()
         rs_cp[s, t] = cp
@@ -200,7 +200,7 @@
         i = held(s, e).index(mask)
         ref = w.at[m, flip(me, mask, k), :, hs(h)]
         cp = pltpu.make_async_remote_copy(
-            src_ref=ref, dst_ref=ref, send_sem=ag_send_sem.at[s, (1 << e) + i], recv_sem=ag_recv.at[s, (1 << e) + i],
+            src_ref=ref, dst_ref=ref, send_sem=ag_send_sem.at[s, (1 << e) + i - 1], recv_sem=ag_recv.at[s, (1 << e) + i - 1],
             device_id=rep(1 << order[s][k - 1 - e]), device_id_type=MESH)
         cp.start()
         ag[s, e, i] = cp
@@ -215,7 +215,7 @@
         mask = held(s, e)[i] ^ (1 << order[s][k - 1 - e])
         ref = w.at[m, flip(me, mask, k), :, hs(h)]
         pltpu.make_async_remote_copy(
-            src_ref=ref, dst_ref=ref, send_sem=ag_send_sem.at[s, (1 << e) + i], recv_sem=ag_recv.at[s, (1 << e) + i],
+            src_ref=ref, dst_ref=ref, send_sem=ag_send_sem.at[s, (1 << e) + i - 1], recv_sem=ag_recv.at[s, (1 << e) + i - 1],
             device_id=rep(1 << order[s][k - 1 - e]), device_id_type=MESH).wait_recv()
         return mask
 
@@ -368,7 +368,7 @@
     def z_copy(c, mask, e, i):
         ref = db.at[c, owner_rows(mask)]
         return pltpu.make_async_remote_copy(
-            src_ref=ref, dst_ref=ref, send_sem=g_send.at[c, (1 << e) + i], recv_sem=g_recv.at[c, (1 << e) + i],
+            src_ref=ref, dst_ref=ref, send_sem=g_send.at[c, (1 << e) + i - 1], recv_sem=g_recv.at[c, (1 << e) + i - 1],
             device_id=zdev(1 << (kz - 1 - e)), device_id_type=MESH)
 
     def z_send_block(c, mask, first):
@@ -534,8 +534,8 @@
         pltpu.VMEM((parts, count, zc), BF16),
         pltpu.VMEM((8, count), F32),
         pltpu.VMEM((groups, 8, count), F32),
-        dma((ns,)), dma((6,)), dma((2, ns)), dma((2, ns, max(n // 4, 1))), dma((2, k, ns)), dma((ns, n)), dma((ns, n)),
-        dma((2, groups)), dma((kz, parts)), dma((kz, parts)), dma((parts, groups)), dma((parts, groups)),
+        dma((ns,)), dma((6,)), dma((2, ns)), dma((2, ns, max(n // 4, 1))), dma((2, max(k - 2, 1), ns)), dma((ns, n - 1)), dma((ns, n - 1)),
+        dma((2, groups)), dma((kz, parts)), dma((kz, parts)), dma((parts, groups - 1)), dma((parts, groups - 1)),
         dma((2, groups)),
     ]
     hbm = pl.BlockSpec(memory_space=pltpu.HBM)

time: 93.1 us -> 92.7 us (level)
  no operation moved by 1% of the time
where the time goes in v4:
time: 92.7 us; the launch traced here: 92.6 us
  Pallas kernels  91.9 us (99%)
    pallas_call x1, Pallas kernels, shards(): pl.pallas_call(functools.partial(kernel, plan), out_shape=(jax.ShapeDtype...  89.2 us
    pallas_call x1, Pallas kernels, shards(): pl.pallas_call(functools.partial(finish, plan), out_shape=(jax.ShapeDtype...  2.73 us

profile of v4, /device:TPU:0, one launch (start us, length us, event | category | flops | bytes accessed | tf_op | source)
XLA Modules:
  0.0 92.6 jit_solution(2169564323063132802)
XLA Ops:
  0.6 89.2 %shard_map.94 = (f32[2,384,512]{2,1,0:T(8,128)S(1)}, f32[2,384,512]{2,1,0:T(8,128)S(1)}, bf16[3072,512]{1,0:T(8,128)(2,1)S(1)}, bf16[4,768,128]{2,1,0:T(8,128)(2...) custom-call(bf16[2,4,2,384,512]{4,3,2,1,0:T(8,128)(2,1)} %bitcast.2, f32[2,384,512]{2,1,0:T(8,128)} %op.1, ...), custom_call_target="tpu_custom_call" | custom-call | tf_op jit(solution)/shard_map/pallas_call | solution.py:542
  89.9 2.7 %shard_map.95 = (f32[2,384,512]{2,1,0:T(8,128)}, f32[2,384,512]{2,1,0:T(8,128)}, bf16[1,3072,512]{2,1,0:T(8,128)(2,1)}) custom-call(f32[2,384,512]{2,1,0:T(8,128)S(1)} %get-tuple-element.9.no, f32[2,384,512]{2,1,0:T(8,128)S(1)} %get-tuple-element.10.nm, bf16[3072,512]{1,0:T(8,128)(2,1)S(1)} %get-tuple-element.11.w0, ...), custom_call_target="tpu_custom_call" | custom-call | tf_op jit(solution)/shard_map/pallas_call | solution.py:559
